TPU v7x, 256 devices: a whole 4x4x8 slice. The times are simulated.
256 devices in a mesh: grp: 2 (over z_hi), gx: 16 (over y, z_lo), gy: 8 (over x, core).
Axes of the slice: x: 4, y: 4, z: 8 (z_hi: 2, z_lo: 4; z = z_hi * 4 + z_lo), core: 2. Of those that a mesh axis runs over, the one named last changes fastest.
Arguments:
- warmth_anomaly: float32 [64, 256, 1024], P('grp', 'gx', 'gy'), may hold values from -6 to 6
- humidity_anomaly: float32 [64, 256, 1024], P('grp', 'gx', 'gy'), may hold values from -6 to 6
- horizontal_line_advective_ratio: float32 [64], replicated, may hold values from -0.5 to 0.5
- vertical_line_advective_ratio: float32 [64], replicated, may hold values from -0.5 to 0.5
- molecular_extinction_coefficient: float32 [112], replicated, may hold values from 0.002 to 0.05
- droplet_extinction_thickness: float32 [112], replicated, may hold values from 0.005 to 0.1
- shortwave_quadrature_share: float32 [112], replicated, may hold values from 0.5 to 5
- longwave_quadrature_share: float32 [112], replicated, may hold values from 0.5 to 5
- overcast_layer_flags: int32 [65536, 64], P(('grp', 'gx', 'gy')), may hold values 0 or 1
- profile_position_within_tile: int32 [128, 512], P('gx', 'gy'), may hold values from 0 to 511, as said below
Outputs:
- temperature_out: float32 [64, 256, 1024], P('grp', 'gx', 'gy')
- moisture_out: float32 [64, 256, 1024], P('grp', 'gx', 'gy')
- warming_rates: float32 [65536, 64], P(('grp', 'gx', 'gy'))
Inputs may be any that keep to these rules, and one draw needn't show every extreme that they name: `profile_position_within_tile`: each tile's block of 8 x 64 entries holds every number from 0 to 511 exactly once.
All inputs are finite; a program needn't handle non-finite values. No bound on the sum of `overcast_layer_flags` on one device may be relied on, other than what follows from the above.
Results may differ from a plain program's by a relative error of at most 0.000092.
Values sent between devices are 32-bit elements; how exact they have to be, the bound alone decides.
A program may use at most 64 MiB of HBM per device.

v0:
```python
import functools
import math

import jax
import jax.numpy as jnp
from jax import lax
from jax.experimental import pallas as pl
from jax.experimental.pallas import tpu as pltpu
from jax.sharding import PartitionSpec as P

SWEEPS = 8
NU_H = 0.15
NU_V = 0.15
HEATING_INTERVAL = 0.5
LEV = 32
ROWS = 16
COLS = 128
H = 8
PAD = 8
XL = LEV + H
XR = ROWS + 2 * H
ALL = XL + 2 * PAD
G = 112
GB = 4
F32 = jnp.float32
MESH = pl.DeviceIdType.MESH
HI = lax.Precision.HIGHEST


def lanes(shape):
    return lax.broadcasted_iota(jnp.int32, shape, len(shape) - 1)


def subs(shape):
    return lax.broadcasted_iota(jnp.int32, shape, len(shape) - 2)


def roll(x, amount, axis=1):
    n = x.shape[axis]
    amount = amount % n
    return x if amount == 0 else pltpu.roll(x, amount, axis)


def kernel(
    sizes,
    cx_ref, cy_ref, k_ref, d_ref, sw_ref, lw_ref,
    t_ref, m_ref, flags_ref, slot_ref,
    to_ref, mo_ref, wr_ref,
    fa, fb, ea, eb, coef, yst, arad, crad, trad, acc, fts, fsend, frecv, a0s, a0r, c0b,
    oh, fc, pws, wrecv, wt, cus, ews, ewl, ewr, eps, epl, epr,
    send, recv,
):
    ng, nx, ny = sizes
    g, x, y = lax.axis_index("grp"), lax.axis_index("gx"), lax.axis_index("gy")
    og = 1 - g
    xn, xp = lax.rem(x + 1, nx), lax.rem(x + nx - 1, nx)
    yn, yp = lax.rem(y + 1, ny), lax.rem(y + ny - 1, ny)
    gf = g.astype(F32)
    peers = [(og, x, y), (g, xn, y), (g, xp, y), (og, xn, y), (og, xp, y), (g, x, yn), (g, x, yp)]

    barrier = pltpu.get_barrier_semaphore()
    for peer in peers:
        pl.semaphore_signal(barrier, inc=1, device_id=peer, device_id_type=MESH)

    def copy(i, src, dst, peer):
        return pltpu.make_async_remote_copy(
            src_ref=src, dst_ref=dst, send_sem=send.at[i], recv_sem=recv.at[i],
            device_id=peer, device_id_type=MESH,
        )

    own = pl.multiple_of(PAD + H * g, 8)

    def place(r, _):
        fa[0, H + r, pl.ds(own, LEV), :] = t_ref[pl.ds(r, LEV, stride=ROWS), :]
        fa[1, H + r, pl.ds(own, LEV), :] = roll(m_ref[pl.ds(r, LEV, stride=ROWS), :], 64)
        return 0

    lax.fori_loop(0, ROWS, place, 0)
    zero8 = jnp.zeros((8, COLS), F32)

    def clear(r, _):
        for buf in (fa, fb):
            for f in range(2):
                buf[f, r, 0:PAD, :] = zero8
                buf[f, r, PAD + XL:ALL, :] = zero8
        for buf in (ea, eb):
            buf[r, 0:PAD, :] = zero8
            buf[r, PAD + XL:ALL, :] = zero8
        return 0

    lax.fori_loop(0, XR, clear, 0)

    def coefs(i, _):
        level = i + 24 * g
        hx, hy = 0.5 * cx_ref[level], 0.5 * cy_ref[level]
        for n, value in enumerate((NU_H - hx, NU_H + hx, NU_H - hy, NU_H + hy)):
            coef[n, pl.ds(i, 1), :] = jnp.full((1, COLS), value, F32)
        return 0

    lax.fori_loop(0, XL, coefs, 0)

    kk = lax.broadcasted_iota(jnp.int32, (2 * COLS, COLS), 0)
    nn = lax.broadcasted_iota(jnp.int32, (2 * COLS, COLS), 1)
    means = []
    for f in range(2):
        shift = 64 * f
        column = (kk + COLS - shift) % COLS
        pick = jnp.where(nn == (kk // COLS) * 64 + column // 2, 0.25, 0.0).astype(F32)
        parts = []
        for q in range(4):
            base = H + 4 * q
            rows = [fa[f, base + n, pl.ds(own, LEV), :] for n in range(4)]
            parts.append(jnp.concatenate([rows[0] + rows[1], rows[2] + rows[3]], axis=1))
        means.append(jnp.dot(jnp.concatenate(parts, axis=0), pick, precision=HI, preferred_element_type=F32))
    heatq = 1.0 + 0.1 * means[0]
    m = means[1]
    absorber = jnp.maximum(m, 0.0) + jnp.log1p(jnp.exp(-jnp.abs(m)))
    for q in range(4):
        for seg in range(2):
            at = pl.ds(4 * seg + q, 16, stride=8)
            low = q * LEV + 16 * seg
            arad[at, :] = absorber[low:low + 16]
            trad[at, :] = heatq[low:low + 16]
    tot_a = arad[0:8, :]
    for s in range(1, 16):
        tot_a = tot_a + arad[8 * s:8 * s + 8, :]
    a0s[...] = tot_a + roll(tot_a, 4, 0)

    fts[...] = flags_ref[...].astype(F32).T
    below = jnp.sum(fts[0:LEV, :], axis=0, keepdims=True)
    fsend[0:LEV, :] = fts[pl.ds(pl.multiple_of(LEV * og, 8), LEV), :]
    fsend[LEV:LEV + 8, :] = jnp.broadcast_to(below * (1.0 - gf), (8, 256))

    pl.semaphore_wait(barrier, len(peers))

    face = pl.multiple_of(PAD + 24 - 16 * g, 8)
    land = pl.multiple_of(PAD + 32 * g, 8)
    lev = pl.ds(own, LEV)
    sends = [
        copy(0, fsend, frecv, (og, x, y)),
        copy(1, a0s, a0r, (og, x, y)),
    ]
    for f in range(2):
        sends.append(copy(2 + f, fa.at[f, pl.ds(ROWS, H), lev, :], fa.at[f, pl.ds(0, H), lev, :], (g, xn, y)))
        sends.append(copy(4 + f, fa.at[f, pl.ds(H, H), lev, :], fa.at[f, pl.ds(H + ROWS, H), lev, :], (g, xp, y)))
    for f in range(2):
        sends.append(copy(6 + f, fa.at[f, pl.ds(H, ROWS), pl.ds(face, H), :], fa.at[f, pl.ds(H, ROWS), pl.ds(land, H), :], (og, x, y)))
        sends.append(copy(8 + f, fa.at[f, pl.ds(ROWS, H), pl.ds(face, H), :], fa.at[f, pl.ds(0, H), pl.ds(land, H), :], (og, xn, y)))
        sends.append(copy(10 + f, fa.at[f, pl.ds(H, H), pl.ds(face, H), :], fa.at[f, pl.ds(H + ROWS, H), pl.ds(land, H), :], (og, xp, y)))
    for c in sends:
        c.start()

    slot = lax.broadcasted_iota(jnp.int32, (512, COLS), 0)
    for q in range(4):
        line = jnp.concatenate([slot_ref[2 * q:2 * q + 1, :], slot_ref[2 * q + 1:2 * q + 2, :]], axis=1)
        oh[:, q * COLS:(q + 1) * COLS] = jnp.where(slot == line, 1.0, 0.0).astype(jnp.bfloat16)

    mine = pl.multiple_of(256 * g, 256)
    theirs = pl.multiple_of(256 * og, 256)
    fc[0:LEV, pl.ds(mine, 256)] = fts[pl.ds(pl.multiple_of(LEV * g, 8), LEV), :]
    fc[LEV:LEV + 8, pl.ds(mine, 256)] = jnp.broadcast_to(below * gf, (8, 256))
    sends[0].wait_recv()
    fc[:, pl.ds(theirs, 256)] = frecv[...]
    placed = jnp.dot(fc[...].astype(jnp.bfloat16), oh[...], preferred_element_type=F32)
    for q in range(4):
        part = placed[:, q * COLS:(q + 1) * COLS]
        for seg in range(2):
            crad[pl.ds(4 * seg + q, 16, stride=8), :] = part[16 * seg:16 * seg + 16]
            c0b[4 * seg + q:4 * seg + q + 1, :] = part[LEV:LEV + 1]
    tot_c = crad[0:8, :]
    for s in range(1, 16):
        tot_c = tot_c + crad[8 * s:8 * s + 8, :]
    second = subs((8, COLS)) >= 4
    sends[1].wait_recv()
    init_a = jnp.where(second, roll(tot_a, 4, 0), 0.0) + gf * a0r[...]
    init_c = jnp.where(second, roll(tot_c, 4, 0), 0.0) + c0b[...]
    a0r[...] = init_a
    c0b[...] = init_c

    scale = -math.log2(math.e)
    acc[...] = jnp.zeros_like(acc)

    def radiate(block, _):
        ks, ds, ls, beams = [], [], [], []
        start_a, start_c = a0r[...], c0b[...]
        for j in range(GB):
            n = block * GB + j
            ks.append(scale * k_ref[n])
            ds.append(scale * d_ref[n])
            ls.append(lw_ref[n])
            beams.append(sw_ref[n] * jnp.exp2(start_a * ks[j] + start_c * ds[j]))
        for s in range(16):
            a, c, q = (ref[8 * s:8 * s + 8, :] for ref in (arad, crad, trad))
            total = acc[8 * s:8 * s + 8, :]
            for j in range(GB):
                e = jnp.exp2(a * ks[j] + c * ds[j])
                total = total + (beams[j] - q * ls[j]) * (1.0 - e)
                beams[j] = beams[j] * e
            acc[8 * s:8 * s + 8, :] = total
        return 0

    lax.fori_loop(0, G // GB, radiate, 0)

    tiles = []
    for q in range(4):
        both = [acc[pl.ds(4 * seg + q, 16, stride=8), :] for seg in range(2)]
        tiles.append(jnp.concatenate(both, axis=0) * (4.0 / G))
    rates = jnp.concatenate(tiles, axis=1)
    stacked = jnp.concatenate(tiles, axis=0)

    kk = lax.broadcasted_iota(jnp.int32, (COLS, 2 * COLS), 0)
    nn = lax.broadcasted_iota(jnp.int32, (COLS, 2 * COLS), 1)
    same = (kk // 64) == (nn // COLS)
    col, src = nn % COLS, kk % 64
    up = jnp.where(src == col // 2, 0.75, jnp.where(src == col // 2 - 1 + 2 * (col % 2), 0.25, 0.0))
    up = jnp.where(same, up, 0.0).astype(F32)
    refined = jnp.dot(stacked, up, precision=HI, preferred_element_type=F32)
    lane = lanes((LEV, COLS))
    packed = jnp.zeros((LEV, COLS), F32)
    inner = []
    for i in range(8):
        q, half = i // 2, i % 2
        line = refined[q * LEV:(q + 1) * LEV, half * COLS:(half + 1) * COLS]
        inner.append(line)
        cus[1 + i] = line
        here = (lane == 2 * i) | (lane == (2 * i - 1) % COLS)
        packed = jnp.where(here, roll(line, 2 * i), packed)
    ews[...] = packed
    ends = [copy(12, ews, ewl, (g, x, yn)), copy(13, ews, ewr, (g, x, yp))]
    for c in ends:
        c.start()

    rest = rates
    total = None
    for _ in range(3):
        piece = rest.astype(jnp.bfloat16)
        rest = rest - piece.astype(F32)
        part = lax.dot_general(piece, oh[...], (((1,), (1,)), ((), ())), preferred_element_type=F32)
        total = part if total is None else total + part
    pws[...] = total
    back = copy(14, pws.at[:, pl.ds(theirs, 256)], wrecv, (og, x, y))
    back.start()
    wt[pl.ds(pl.multiple_of(LEV * g, 8), LEV), :] = pws[:, pl.ds(mine, 256)]

    for c in ends:
        c.wait_recv()
    left, right = ewl[...] * (1.0 / 3.0), ewr[...] * (1.0 / 3.0)
    for i in range(8):
        line = cus[1 + i]
        line = line + jnp.where(lane == 0, roll(left, 1 - 2 * i), 0.0)
        line = line + jnp.where(lane == COLS - 1, roll(right, COLS - 1 - 2 * i), 0.0)
        cus[1 + i] = line
    lines = [copy(15, cus.at[8], cus.at[0], (g, xn, y)), copy(16, cus.at[1], cus.at[9], (g, xp, y))]
    for c in lines:
        c.start()

    for c in sends[2:]:
        c.wait_recv()
    lane = lanes((XL, COLS))
    outer = (lane < 8) | (lane >= COLS - 8)
    ext = pl.ds(PAD, XL)

    def pack(t, _):
        total = None
        for j in range(4):
            row = 4 * t + j
            edge = jnp.where(outer, fa[0, row, ext, :], fa[1, row, ext, :])
            edge = roll(edge, 16 * j)
            seat = (lane + COLS + 8 - 16 * j) % 64 < 16
            total = edge if total is None else jnp.where(seat, edge, total)
        eps[t] = total
        return 0

    lax.fori_loop(0, XR // 4, pack, 0)
    edges = [copy(17, eps, epl, (g, x, yn)), copy(18, eps, epr, (g, x, yp))]
    for c in edges:
        c.start()
    for c in edges:
        c.wait_recv()
    from_left = (lane + 8) % 16 < 8

    def unpack(t, _):
        both = jnp.where(from_left, epl[t], epr[t])
        for j in range(4):
            ea[4 * t + j, ext, :] = roll(both, -16 * j)
        return 0

    lax.fori_loop(0, XR // 4, unpack, 0)
    for c in sends[2:]:
        c.wait_send()

    at_first, at_last = lane == 0, lane == COLS - 1
    mid_first, mid_last = lane == 64, lane == 63
    above, below_, = pl.ds(PAD - 1, XL), pl.ds(PAD + 1, XL)

    def step(src, esrc, r):
        an, ap, bn, bp = (coef[n] for n in range(4))

        def update(centre, nxt, prv, cols_n, cols_p, up_, down):
            return (
                (1.0 - 4.0 * NU_H - 2.0 * NU_V) * centre + an * nxt + ap * prv
                + bn * roll(cols_n, -1) + bp * roll(cols_p, 1) + NU_V * (up_ + down)
            )

        c0, c1, ce = src[0, r, ext, :], src[1, r, ext, :], esrc[r, ext, :]
        new0 = update(
            c0, src[0, r + 1, ext, :], src[0, r - 1, ext, :],
            jnp.where(at_first, ce, c0), jnp.where(at_last, ce, c0),
            src[0, r, above, :], src[0, r, below_, :],
        )
        new1 = update(
            c1, src[1, r + 1, ext, :], src[1, r - 1, ext, :],
            jnp.where(mid_first, ce, c1), jnp.where(mid_last, ce, c1),
            src[1, r, above, :], src[1, r, below_, :],
        )
        newe = update(
            ce, esrc[r + 1, ext, :], esrc[r - 1, ext, :],
            jnp.where(at_first, c0, jnp.where(mid_first, c1, ce)),
            jnp.where(at_last, c0, jnp.where(mid_last, c1, ce)),
            esrc[r, above, :], esrc[r, below_, :],
        )
        return new0, new1, newe

    bufs = [(fa, ea), (fb, eb)]
    for sweep in range(1, SWEEPS + 1):
        (src, esrc), (dst, edst) = bufs[(sweep - 1) % 2], bufs[sweep % 2]

        def row(r, _, src=src, esrc=esrc, dst=dst, edst=edst):
            new0, new1, newe = step(src, esrc, r)
            dst[0, r, ext, :] = new0
            dst[1, r, ext, :] = new1
            edst[r, ext, :] = newe
            return 0

        lax.fori_loop(sweep, XR - sweep, row, 0)

    for c in lines:
        c.wait_recv()

    def finish(i, _):
        for half in range(2):
            r = 2 * i + half
            heat = 0.75 * cus[1 + i] + 0.25 * cus[i + 2 * half]
            to_ref[pl.ds(r, LEV, stride=ROWS), :] = fa[0, H + r, pl.ds(own, LEV), :] + HEATING_INTERVAL * heat
            mo_ref[pl.ds(r, LEV, stride=ROWS), :] = roll(fa[1, H + r, pl.ds(own, LEV), :], 64)
        return 0

    lax.fori_loop(0, ROWS // 2, finish, 0)

    back.wait_recv()
    wt[pl.ds(pl.multiple_of(LEV * og, 8), LEV), :] = wrecv[...]
    wr_ref[...] = wt[...].T
    for c in [*sends[:2], *ends, back, *lines, *edges]:
        c.wait_send()


def body(sizes, t, m, cx, cy, k, d, sw, lw, flags, slots):
    smem = pl.BlockSpec(memory_space=pltpu.SMEM)
    vmem = pl.BlockSpec(memory_space=pltpu.VMEM)
    flat = (LEV * ROWS, COLS)
    scratch = [
        pltpu.VMEM((2, XR, ALL, COLS), F32),
        pltpu.VMEM((2, XR, ALL, COLS), F32),
        pltpu.VMEM((XR, ALL, COLS), F32),
        pltpu.VMEM((XR, ALL, COLS), F32),
        pltpu.VMEM((4, XL, COLS), F32),
        pltpu.VMEM((8, COLS), F32),
        pltpu.VMEM((128, COLS), F32),
        pltpu.VMEM((128, COLS), F32),
        pltpu.VMEM((128, COLS), F32),
        pltpu.VMEM((128, COLS), F32),
        pltpu.VMEM((2 * LEV, 256), F32),
        pltpu.VMEM((LEV + 8, 256), F32),
        pltpu.VMEM((LEV + 8, 256), F32),
        pltpu.VMEM((8, COLS), F32),
        pltpu.VMEM((8, COLS), F32),
        pltpu.VMEM((8, COLS), F32),
        pltpu.VMEM((512, 512), jnp.bfloat16),
        pltpu.VMEM((LEV + 8, 512), F32),
        pltpu.VMEM((LEV, 512), F32),
        pltpu.VMEM((LEV, 256), F32),
        pltpu.VMEM((2 * LEV, 256), F32),
        pltpu.VMEM((10, LEV, COLS), F32),
        pltpu.VMEM((LEV, COLS), F32),
        pltpu.VMEM((LEV, COLS), F32),
        pltpu.VMEM((LEV, COLS), F32),
        pltpu.VMEM((XR // 4, XL, COLS), F32),
        pltpu.VMEM((XR // 4, XL, COLS), F32),
        pltpu.VMEM((XR // 4, XL, COLS), F32),
        pltpu.SemaphoreType.DMA((19,)),
        pltpu.SemaphoreType.DMA((19,)),
    ]
    to, mo, wr = pl.pallas_call(
        functools.partial(kernel, sizes),
        out_shape=(
            jax.ShapeDtypeStruct(flat, F32),
            jax.ShapeDtypeStruct(flat, F32),
            jax.ShapeDtypeStruct((256, 2 * LEV), F32),
        ),
        in_specs=[smem] * 6 + [vmem] * 4,
        out_specs=(vmem, vmem, vmem),
        scratch_shapes=scratch,
        compiler_params=pltpu.CompilerParams(
            collective_id=0, has_side_effects=True, vmem_limit_bytes=32 * 1024 * 1024
        ),
    )(cx, cy, k, d, sw, lw, t.reshape(flat), m.reshape(flat), flags, slots)
    return to.reshape(t.shape), mo.reshape(t.shape), wr


def solution(mesh):
    sizes = tuple(mesh.shape[a] for a in ("grp", "gx", "gy"))
    in_specs = (
        P("grp", "gx", "gy"), P("grp", "gx", "gy"),
        P(), P(), P(), P(), P(), P(),
        P(("grp", "gx", "gy"), None), P("gx", "gy"),
    )
    out_specs = (P("grp", "gx", "gy"), P("grp", "gx", "gy"), P(("grp", "gx", "gy"), None))
    return jax.shard_map(
        functools.partial(body, sizes), mesh=mesh, in_specs=in_specs, out_specs=out_specs, check_vma=False
    )
```

profile of v0, /device:TPU:1, one launch (start us, length us, event | category | flops | bytes accessed | tf_op | source)
XLA Modules:
  0.0 69.0 jit_solution(2998269105260412485)
XLA Ops:
  0.6 0.0 copy-start.2
  0.6 0.0 copy-start.3
  0.7 0.0 copy-start.4
  0.7 0.0 copy-start.5
  0.7 0.0 copy-start.6
  0.7 0.0 copy-start.7
  0.7 0.0 copy-start.8
  0.7 1.0 %copy.13.flags_ref = s32[256,64]{1,0:T(8,128)S(1)} copy(s32[256,64]{0,1:T(8,128)} %param.18) | data formatting | bytes 131072 | tf_op args[8]
  1.7 0.0 copy-done.2
  1.7 0.0 copy-done.3
  1.7 0.0 copy-done.4
  1.7 0.0 copy-done.5
  1.7 0.0 copy-done.6
  1.7 0.0 copy-done.7
  1.7 0.0 copy-done.8
  1.7 0.0 copy-start
  1.8 0.9 %copy-done = f32[32,16,128]{2,1,0:T(8,128)S(1)} copy-done((f32[32,16,128]{2,1,0:T(8,128)S(1)}, f32[32,16,128]{2,1,0:T(8,128)}, u32[]{:S(2)}) %copy-start) | copy-done | bytes 262168
  2.7 0.0 copy-start.1
  2.7 0.9 %copy-done.1 = f32[32,16,128]{2,1,0:T(8,128)S(1)} copy-done((f32[32,16,128]{2,1,0:T(8,128)S(1)}, f32[32,16,128]{2,1,0:T(8,128)}, u32[]{:S(2)}) %copy-start.1) | copy-done | bytes 262168
  3.7 63.3 %shard_map.121 = (f32[512,128]{1,0:T(8,128)S(1)}, f32[512,128]{1,0:T(8,128)S(1)}, f32[256,64]{1,0:T(8,128)S(1)}) custom-call(f32[64]{0:T(128)S(1)} %copy-done.3, f32[64]{0:T(128)S(1)} %copy-done.4, f32[112]{0:T(128)S(1)} %copy-done.5, f32[112]{0:T(128)S(1)} %copy-done.6, f32[112]{0:T(128)S(1)} %copy-done.7, f32[112]{0:T(128)S(1)} %copy-done.8, ...), custom_call_target="tpu_custom_call" | custom-call | tf_op jit(solution)/shard_map/pallas_call | solution.py:393
  66.9 0.7 %copy.14 = f32[256,64]{0,1:T(8,128)} copy(f32[256,64]{1,0:T(8,128)S(1)} %get-tuple-element.11) | data formatting | bytes 131072
  67.6 0.7 %copy.17 = f32[32,16,128]{2,1,0:T(8,128)} copy(f32[32,16,128]{2,1,0:T(8,128)S(1)} %bitcast.7) | data formatting | bytes 524288
  68.3 0.7 %copy.18 = f32[32,16,128]{2,1,0:T(8,128)} copy(f32[32,16,128]{2,1,0:T(8,128)S(1)} %bitcast.6) | data formatting | bytes 524288
Async XLA Ops:
  0.6 1.0 %copy-start.2 = (s32[8,64]{1,0:T(8,128)S(1)}, s32[8,64]{1,0:T(8,128)}, u32[]{:S(2)}) copy-start(s32[8,64]{1,0:T(8,128)} %slot_ref.1) | copy-start | bytes 6148
  0.6 1.0 %copy-start.3 = (f32[64]{0:T(128)S(1)}, f32[64]{0:T(128)}, u32[]{:S(2)}) copy-start(f32[64]{0:T(128)} %cx_ref.1) | copy-start | bytes 772
  0.7 1.0 %copy-start.4 = (f32[64]{0:T(128)S(1)}, f32[64]{0:T(128)}, u32[]{:S(2)}) copy-start(f32[64]{0:T(128)} %cy_ref.1) | copy-start | bytes 772
  0.7 1.0 %copy-start.5 = (f32[112]{0:T(128)S(1)}, f32[112]{0:T(128)}, u32[]{:S(2)}) copy-start(f32[112]{0:T(128)} %k_ref.1) | copy-start | bytes 1348
  0.7 1.0 %copy-start.6 = (f32[112]{0:T(128)S(1)}, f32[112]{0:T(128)}, u32[]{:S(2)}) copy-start(f32[112]{0:T(128)} %d_ref.1) | copy-start | bytes 1348
  0.7 1.0 %copy-start.7 = (f32[112]{0:T(128)S(1)}, f32[112]{0:T(128)}, u32[]{:S(2)}) copy-start(f32[112]{0:T(128)} %sw_ref.1) | copy-start | bytes 1348
  0.7 1.0 %copy-start.8 = (f32[112]{0:T(128)S(1)}, f32[112]{0:T(128)}, u32[]{:S(2)}) copy-start(f32[112]{0:T(128)} %lw_ref.1) | copy-start | bytes 1348
  1.7 1.0 %copy-start = (f32[32,16,128]{2,1,0:T(8,128)S(1)}, f32[32,16,128]{2,1,0:T(8,128)}, u32[]{:S(2)}) copy-start(f32[32,16,128]{2,1,0:T(8,128)} %param.10) | copy-start | bytes 786436
  2.7 0.9 %copy-start.1 = (f32[32,16,128]{2,1,0:T(8,128)S(1)}, f32[32,16,128]{2,1,0:T(8,128)}, u32[]{:S(2)}) copy-start(f32[32,16,128]{2,1,0:T(8,128)} %param.11) | copy-start | bytes 786436
where the time goes:
time: 69.2 us; the launch traced here: 69 us
  Pallas kernels  63.3 us (91%)
  local copies, waits for them, and re-layouts  5.01 us (7%)
  between operations  0.77 us (1%)
    pallas_call x1, Pallas kernels, body(): pl.pallas_call(functools.partial(kernel, sizes), out_shape=(jax.ShapeDtyp...  63.3 us
    unnamed x22, local copies, waits for them, and re-layouts  5.01 us

commit v1 on v0

v1 whole, which is shorter than its diff:
```python
import functools
import math

import jax
import jax.numpy as jnp
from jax import lax
from jax.experimental import pallas as pl
from jax.experimental.pallas import tpu as pltpu
from jax.sharding import PartitionSpec as P

SWEEPS = 8
NU_H = 0.15
NU_V = 0.15
HEATING_INTERVAL = 0.5
LEV = 32
ROWS = 16
COLS = 128
H = 8
XR = ROWS + 2 * H
UP, OWN, DOWN, ALL = 8, 16, 48, 64
G = 112
GB = 4
F32 = jnp.float32
MESH = pl.DeviceIdType.MESH
HI = lax.Precision.HIGHEST


def lanes(shape):
    return lax.broadcasted_iota(jnp.int32, shape, len(shape) - 1)


def subs(shape):
    return lax.broadcasted_iota(jnp.int32, shape, len(shape) - 2)


def roll(x, amount, axis=1):
    n = x.shape[axis]
    amount = amount % n
    return x if amount == 0 else pltpu.roll(x, amount, axis)


def kernel(
    sizes,
    cx_hbm, cy_hbm, k_hbm, d_hbm, sw_hbm, lw_hbm,
    t_hbm, m_hbm, flags_hbm, slot_hbm,
    to_ref, mo_ref, wr_ref,
    cx_ref, cy_ref, k_ref, d_ref, sw_ref, lw_ref,
    tin, min_, fin, sin,
    fs, es, coef, arad, crad, trad, acc, fsend, frecv, a0r, c0b,
    oh, fc, pws, wrecv, cus, ews, ewl, ewr,
    eos, eol, eor, els, ell, elr, ehs, ehl, ehr, hst, hland,
    load, send, recv,
):
    ng, nx, ny = sizes
    g, x, y = lax.axis_index("grp"), lax.axis_index("gx"), lax.axis_index("gy")
    og = 1 - g
    xn, xp = lax.rem(x + 1, nx), lax.rem(x + nx - 1, nx)
    yn, yp = lax.rem(y + 1, ny), lax.rem(y + ny - 1, ny)
    gf = g.astype(F32)
    peers = [(og, x, y), (g, xn, y), (g, xp, y), (og, xn, y), (og, xp, y), (g, x, yn), (g, x, yp)]

    barrier = pltpu.get_barrier_semaphore()
    for peer in peers:
        pl.semaphore_signal(barrier, inc=1, device_id=peer, device_id_type=MESH)
    loads = [
        pltpu.make_async_copy(src, dst, load.at[n])
        for n, (src, dst) in enumerate((
            (m_hbm, min_), (t_hbm, tin), (flags_hbm, fin), (slot_hbm, sin), (cx_hbm, cx_ref),
            (cy_hbm, cy_ref), (k_hbm, k_ref), (d_hbm, d_ref), (sw_hbm, sw_ref), (lw_hbm, lw_ref),
        ))
    ]
    for c in loads:
        c.start()

    def copy(i, src, dst, peer):
        return pltpu.make_async_remote_copy(
            src_ref=src, dst_ref=dst, send_sem=send.at[i], recv_sem=recv.at[i],
            device_id=peer, device_id_type=MESH,
        )

    own = pl.ds(OWN, LEV)
    zero8 = jnp.zeros((8, COLS), F32)

    for c in loads[:2]:
        c.wait()

    def place(b, _):
        for j in range(4):
            r = 4 * b + j
            fs[0, 0, H + r, own, :] = tin[pl.ds(r, LEV, stride=ROWS), :]
            fs[0, 1, H + r, own, :] = roll(min_[pl.ds(r, LEV, stride=ROWS), :], 64)
        return 0

    lax.fori_loop(0, ROWS // 4, place, 0)
    for c in loads[2:]:
        c.wait()
    pl.semaphore_wait(barrier, len(peers))

    face = pl.ds(pl.multiple_of(DOWN - 8 - 24 * g, 8), H)
    land = pl.ds(pl.multiple_of(8 + 40 * g, 8), H)
    first, last, mid = pl.ds(H, H), pl.ds(ROWS, H), pl.ds(H, ROWS)
    low, high = pl.ds(0, H), pl.ds(H + ROWS, H)
    levels_in = [
        copy(4, fs.at[0, :, mid, face, :], fs.at[0, :, mid, land, :], (og, x, y)),
        copy(5, fs.at[0, :, last, face, :], fs.at[0, :, low, land, :], (og, xn, y)),
        copy(6, fs.at[0, :, first, face, :], fs.at[0, :, high, land, :], (og, xp, y)),
    ]
    rows_low = copy(2, fs.at[0, :, last, own, :], fs.at[0, :, low, own, :], (g, xn, y))
    rows_high = copy(3, hst, hland, (g, xp, y))
    for c in levels_in:
        c.start()

    for part in range(2):
        for r in range(H):
            hst[H * part + r] = fs[0, part, H + r, own, :]

    lane = lanes((LEV, COLS))
    outer = (lane < 8) | (lane >= COLS - 8)
    seats = [(lane + COLS + 8 - 16 * j) % 64 < 16 for j in range(4)]
    from_left = (lane + 8) % 16 < 8

    def pack(row, at=own, n=LEV):
        total = None
        for j in range(4):
            edge = jnp.where(outer[:n], fs[0, 0, row + j, at, :], fs[0, 1, row + j, at, :])
            edge = roll(edge, 16 * j)
            total = edge if total is None else jnp.where(seats[j][:n], edge, total)
        return total

    for t in range(4):
        eos[t] = pack(H + 4 * t)
    edges_own = [copy(7, eos, eol, (g, x, yn)), copy(8, eos, eor, (g, x, yp))]
    for c in edges_own:
        c.start()

    kk = lax.broadcasted_iota(jnp.int32, (2 * COLS, COLS), 0)
    nn = lax.broadcasted_iota(jnp.int32, (2 * COLS, COLS), 1)
    means = []
    for f in range(2):
        column = (kk + COLS - 64 * f) % COLS
        pick = jnp.where(nn == (kk // COLS) * 64 + column // 2, 0.25, 0.0).astype(F32)
        parts = []
        for q in range(4):
            rows = [fs[0, f, H + 4 * q + n, own, :] for n in range(4)]
            parts.append(jnp.concatenate([rows[0] + rows[1], rows[2] + rows[3]], axis=1))
        means.append(jnp.dot(jnp.concatenate(parts, axis=0), pick, precision=HI, preferred_element_type=F32))
    heatq = 1.0 + 0.1 * means[0]
    m = means[1]
    absorber = jnp.maximum(m, 0.0) + jnp.log1p(jnp.exp(-jnp.abs(m)))
    for q in range(4):
        for seg in range(2):
            at = pl.ds(4 * seg + q, 16, stride=8)
            low = q * LEV + 16 * seg
            arad[at, :] = absorber[low:low + 16]
            trad[at, :] = heatq[low:low + 16]
    tot_a = arad[0:8, :]
    for s in range(1, 16):
        tot_a = tot_a + arad[8 * s:8 * s + 8, :]
    below = jnp.sum(fin[0:LEV, :].astype(F32), axis=0, keepdims=True)
    whole_a = tot_a + roll(tot_a, 4, 0)
    fsend[0:LEV, :] = fin[pl.ds(pl.multiple_of(LEV * og, 8), LEV), :].astype(F32)
    fsend[LEV:LEV + 8, 0:COLS] = whole_a
    fsend[LEV:LEV + 8, COLS:2 * COLS] = whole_a
    fsend[LEV:LEV + 1, COLS:2 * COLS] = below[:, 0:COLS]
    fsend[LEV + 1:LEV + 2, COLS:2 * COLS] = below[:, COLS:256]
    clouds = copy(0, fsend, frecv, (og, x, y))
    for c in [clouds, rows_low]:
        c.start()

    for c in edges_own:
        c.wait_recv()
    for t in range(4):
        whole = jnp.where(from_left, eol[t], eor[t])
        if t < 2:
            hst[2 * H + t] = whole
        for j in range(4):
            es[0, H + 4 * t + j, own, :] = roll(whole, -16 * j)
    rows_high.start()

    dead = pl.ds(pl.multiple_of(8 + 40 * g, 8), H)
    zero8 = jnp.zeros((8, COLS), F32)

    def clear(r, _):
        for n in range(SWEEPS):
            for part in range(2):
                fs[n, part, r, dead, :] = zero8
            es[n, r, dead, :] = zero8
        return 0

    lax.fori_loop(0, XR, clear, 0)

    def coefs(i, _):
        level = i + 24 * g
        hx, hy = 0.5 * cx_ref[level], 0.5 * cy_ref[level]
        for n, value in enumerate((NU_H - hx, NU_H + hx, NU_H - hy, NU_H + hy)):
            coef[n, pl.ds(OWN - 8 * g + i, 1), :] = jnp.full((1, COLS), value, F32)
        return 0

    lax.fori_loop(0, LEV + H, coefs, 0)


    slot = lax.broadcasted_iota(jnp.int32, (512, COLS), 0)
    for q in range(4):
        line = jnp.concatenate([sin[2 * q:2 * q + 1, :], sin[2 * q + 1:2 * q + 2, :]], axis=1)
        oh[:, q * COLS:(q + 1) * COLS] = jnp.where(slot == line, 1.0, 0.0).astype(jnp.bfloat16)

    mine = pl.multiple_of(256 * g, 256)
    theirs = pl.multiple_of(256 * og, 256)
    def advance(sweep, lo, n, row0, count):
        here, above, beneath = pl.ds(lo, n), pl.ds(lo - 1, n), pl.ds(lo + 1, n)
        lane = lanes((n, COLS))
        at_first, at_last = lane == 0, lane == COLS - 1
        mid_first, mid_last = lane == 64, lane == 63
        p = sweep - 1
        an, ap, bn, bp = (coef[c, here, :] for c in range(4))

        def update(centre, nxt, prv, cols_n, cols_p, up_, down):
            return (
                (1.0 - 4.0 * NU_H - 2.0 * NU_V) * centre + an * nxt + ap * prv
                + bn * roll(cols_n, -1) + bp * roll(cols_p, 1) + NU_V * (up_ + down)
            )

        for j in range(count):
            r = row0 + j
            c0, c1, ce = fs[p, 0, r, here, :], fs[p, 1, r, here, :], es[p, r, here, :]
            fs[sweep, 0, r, here, :] = update(
                c0, fs[p, 0, r + 1, here, :], fs[p, 0, r - 1, here, :],
                jnp.where(at_first, ce, c0), jnp.where(at_last, ce, c0),
                fs[p, 0, r, above, :], fs[p, 0, r, beneath, :],
            )
            fs[sweep, 1, r, here, :] = update(
                c1, fs[p, 1, r + 1, here, :], fs[p, 1, r - 1, here, :],
                jnp.where(mid_first, ce, c1), jnp.where(mid_last, ce, c1),
                fs[p, 1, r, above, :], fs[p, 1, r, beneath, :],
            )
            es[sweep, r, here, :] = update(
                ce, es[p, r + 1, here, :], es[p, r - 1, here, :],
                jnp.where(at_first, c0, jnp.where(mid_first, c1, ce)),
                jnp.where(at_last, c0, jnp.where(mid_last, c1, ce)),
                es[p, r, above, :], es[p, r, beneath, :],
            )

    def blocks(sweep, lo, n, row0, count, each):
        def block(b, _):
            advance(sweep, lo, n, row0 + b * each, each)
            return 0

        lax.fori_loop(0, count // each, block, 0)

    clouds.wait_recv()
    fc[0:LEV, pl.ds(mine, 256)] = fin[pl.ds(pl.multiple_of(LEV * g, 8), LEV), :].astype(F32)
    fc[0:LEV, pl.ds(theirs, 256)] = frecv[0:LEV, :]
    fc[LEV:LEV + 8, pl.ds(mine, 256)] = jnp.broadcast_to(below * gf, (8, 256))
    count = jnp.concatenate([frecv[LEV:LEV + 1, COLS:256], frecv[LEV + 1:LEV + 2, COLS:256]], axis=1)
    fc[LEV:LEV + 8, pl.ds(theirs, 256)] = jnp.broadcast_to(count * gf, (8, 256))
    placed = jnp.dot(fc[...].astype(jnp.bfloat16), oh[...], preferred_element_type=F32)
    for q in range(4):
        part = placed[:, q * COLS:(q + 1) * COLS]
        for seg in range(2):
            crad[pl.ds(4 * seg + q, 16, stride=8), :] = part[16 * seg:16 * seg + 16]
            c0b[4 * seg + q:4 * seg + q + 1, :] = part[LEV:LEV + 1]
    tot_c = crad[0:8, :]
    for s in range(1, 16):
        tot_c = tot_c + crad[8 * s:8 * s + 8, :]
    second = subs((8, COLS)) >= 4
    init_a = jnp.where(second, roll(tot_a, 4, 0), 0.0) + gf * frecv[LEV:LEV + 8, 0:COLS]
    init_c = jnp.where(second, roll(tot_c, 4, 0), 0.0) + c0b[...]
    a0r[...] = init_a
    c0b[...] = init_c

    scale = -math.log2(math.e)
    acc[...] = jnp.zeros_like(acc)

    def radiate(block, _):
        ks, ds, ls, beams = [], [], [], []
        start_a, start_c = a0r[...], c0b[...]
        for j in range(GB):
            n = block * GB + j
            ks.append(scale * k_ref[n])
            ds.append(scale * d_ref[n])
            ls.append(lw_ref[n])
            beams.append(sw_ref[n] * jnp.exp2(start_a * ks[j] + start_c * ds[j]))
        for s in range(16):
            a, c, q = (ref[8 * s:8 * s + 8, :] for ref in (arad, crad, trad))
            total = acc[8 * s:8 * s + 8, :]
            for j in range(GB):
                e = jnp.exp2(a * ks[j] + c * ds[j])
                total = total + (beams[j] - q * ls[j]) * (1.0 - e)
                beams[j] = beams[j] * e
            acc[8 * s:8 * s + 8, :] = total
        return 0

    lax.fori_loop(0, G // GB, radiate, 0)

    tiles = []
    for q in range(4):
        both = [acc[pl.ds(4 * seg + q, 16, stride=8), :] for seg in range(2)]
        tiles.append(jnp.concatenate(both, axis=0) * (4.0 / G))
    rates = jnp.concatenate(tiles, axis=1)
    stacked = jnp.concatenate(tiles, axis=0)

    kk = lax.broadcasted_iota(jnp.int32, (COLS, 2 * COLS), 0)
    nn = lax.broadcasted_iota(jnp.int32, (COLS, 2 * COLS), 1)
    same = (kk // 64) == (nn // COLS)
    col, src = nn % COLS, kk % 64
    up = jnp.where(src == col // 2, 0.75, jnp.where(src == col // 2 - 1 + 2 * (col % 2), 0.25, 0.0))
    up = jnp.where(same, up, 0.0).astype(F32)
    refined = jnp.dot(stacked, up, precision=HI, preferred_element_type=F32)
    packed = jnp.zeros((LEV, COLS), F32)
    for i in range(8):
        q, half = i // 2, i % 2
        line = refined[q * LEV:(q + 1) * LEV, half * COLS:(half + 1) * COLS]
        cus[1 + i] = line
        here = (lane == 2 * i) | (lane == (2 * i - 1) % COLS)
        packed = jnp.where(here, roll(line, 2 * i), packed)
    ews[...] = packed
    ends = [copy(12, ews, ewl, (g, x, yn)), copy(13, ews, ewr, (g, x, yp))]
    for c in ends:
        c.start()

    rest = rates
    total = None
    for _ in range(3):
        piece = rest.astype(jnp.bfloat16)
        rest = rest - piece.astype(F32)
        part = lax.dot_general(piece, oh[...], (((1,), (1,)), ((), ())), preferred_element_type=F32)
        total = part if total is None else total + part
    pws[...] = total
    back = copy(14, pws.at[:, pl.ds(theirs, 256)], wrecv, (og, x, y))
    back.start()
    wr_ref[pl.ds(pl.multiple_of(LEV * g, 8), LEV), :] = pws[:, pl.ds(mine, 256)]

    for c in levels_in:
        c.wait_recv()
    arrived = pl.ds(pl.multiple_of(DOWN - 40 * g, 8), H)

    def pack_levels(t, _):
        els[t] = pack(4 * t, arrived, H)
        return 0

    lax.fori_loop(0, XR // 4, pack_levels, 0)
    edges_lev = [copy(1, els, ell, (g, x, yn)), copy(11, els, elr, (g, x, yp))]
    for c in edges_lev:
        c.start()

    edge_rows = []

    def offer():
        for t in range(2):
            ehs[t] = pack(4 * t)
        for i, dst, peer in ((9, ehl, (g, x, yn)), (10, ehr, (g, x, yp))):
            edge_rows.append(copy(i, ehs, dst, peer))
            edge_rows[-1].start()

    def take():
        for c in edge_rows:
            c.wait_recv()
        for t in range(2):
            whole = jnp.where(from_left, ehl[t], ehr[t])
            for j in range(4):
                es[0, 4 * t + j, own, :] = roll(whole, -16 * j)

    def sweep_side(n):
        for sweep in range(1, SWEEPS + 1):
            advance(sweep, lo, LEV + H, XR - sweep - H if n else sweep, H)

    rows_low.wait_recv()
    offer()

    for c in ends:
        c.wait_recv()
    left, right = ewl[...] * (1.0 / 3.0), ewr[...] * (1.0 / 3.0)
    for i in range(8):
        line = cus[1 + i]
        line = line + jnp.where(lane == 0, roll(left, 1 - 2 * i), 0.0)
        line = line + jnp.where(lane == COLS - 1, roll(right, COLS - 1 - 2 * i), 0.0)
        cus[1 + i] = line
    lines = [copy(15, cus.at[8], cus.at[0], (g, xn, y)), copy(16, cus.at[1], cus.at[9], (g, xp, y))]
    for c in lines:
        c.start()

    for c in edges_lev:
        c.wait_recv()

    def settle(t, _):
        whole = jnp.where(from_left[:H], ell[t], elr[t])
        for j in range(4):
            es[0, 4 * t + j, arrived, :] = roll(whole, -16 * j)
        return 0

    lax.fori_loop(0, XR // 4, settle, 0)
    lo = pl.multiple_of(OWN - 8 * g, 8)

    for sweep in range(1, SWEEPS):
        count = ROWS - 2 * sweep
        blocks(sweep, lo, LEV + H, H + sweep, count, {14: 7, 12: 6, 10: 5, 8: 4, 6: 6, 4: 4, 2: 2}[count])
    take()
    sweep_side(0)
    rows_high.wait_recv()
    for r in range(H):
        for part in range(2):
            fs[0, part, H + ROWS + r, own, :] = hland[H * part + r]
    for t in range(2):
        whole = hland[2 * H + t]
        for j in range(4):
            es[0, H + ROWS + 4 * t + j, own, :] = roll(whole, -16 * j)
    sweep_side(1)

    for c in lines:
        c.wait_recv()

    def finish(i, _):
        for half in range(2):
            r = 2 * i + half
            heat = 0.75 * cus[1 + i] + 0.25 * cus[i + 2 * half]
            to_ref[pl.ds(r, LEV, stride=ROWS), :] = fs[SWEEPS, 0, H + r, own, :] + HEATING_INTERVAL * heat
            mo_ref[pl.ds(r, LEV, stride=ROWS), :] = roll(fs[SWEEPS, 1, H + r, own, :], 64)
        return 0

    lax.fori_loop(0, ROWS // 2, finish, 0)

    back.wait_recv()
    wr_ref[pl.ds(pl.multiple_of(LEV * og, 8), LEV), :] = wrecv[...]
    for c in [clouds, rows_low, rows_high, *levels_in, *edges_own, *edge_rows, *edges_lev, *ends, back, *lines]:
        c.wait_send()


def write_out(*refs):
    copies = [pltpu.make_async_copy(refs[n], refs[3 + n], refs[6].at[n]) for n in range(3)]
    for c in copies:
        c.start()
    for c in copies:
        c.wait()


def body(sizes, t, m, cx, cy, k, d, sw, lw, flags, slots):
    vmem = pl.BlockSpec(memory_space=pltpu.VMEM)
    hbm = pl.BlockSpec(memory_space=pltpu.HBM)
    flat = (LEV * ROWS, COLS)
    scratch = [
        *[pltpu.SMEM((n,), F32) for n in (64, 64, G, G, G, G)],
        pltpu.VMEM(flat, F32),
        pltpu.VMEM(flat, F32),
        pltpu.VMEM((2 * LEV, 256), jnp.int32),
        pltpu.VMEM((8, 64), jnp.int32),
        pltpu.VMEM((SWEEPS + 1, 2, XR, ALL, COLS), F32),
        pltpu.VMEM((SWEEPS + 1, XR, ALL, COLS), F32),
        pltpu.VMEM((4, ALL, COLS), F32),
        pltpu.VMEM((128, COLS), F32),
        pltpu.VMEM((128, COLS), F32),
        pltpu.VMEM((128, COLS), F32),
        pltpu.VMEM((128, COLS), F32),
        pltpu.VMEM((LEV + 8, 256), F32),
        pltpu.VMEM((LEV + 8, 256), F32),
        pltpu.VMEM((8, COLS), F32),
        pltpu.VMEM((8, COLS), F32),
        pltpu.VMEM((512, 512), jnp.bfloat16),
        pltpu.VMEM((LEV + 8, 512), F32),
        pltpu.VMEM((LEV, 512), F32),
        pltpu.VMEM((LEV, 256), F32),
        pltpu.VMEM((10, LEV, COLS), F32),
        pltpu.VMEM((LEV, COLS), F32),
        pltpu.VMEM((LEV, COLS), F32),
        pltpu.VMEM((LEV, COLS), F32),
        pltpu.VMEM((4, LEV, COLS), F32),
        pltpu.VMEM((4, LEV, COLS), F32),
        pltpu.VMEM((4, LEV, COLS), F32),
        pltpu.VMEM((8, H, COLS), F32),
        pltpu.VMEM((8, H, COLS), F32),
        pltpu.VMEM((8, H, COLS), F32),
        pltpu.VMEM((2, LEV, COLS), F32),
        pltpu.VMEM((2, LEV, COLS), F32),
        pltpu.VMEM((2, LEV, COLS), F32),
        pltpu.VMEM((2 * H + 2, LEV, COLS), F32),
        pltpu.VMEM((2 * H + 2, LEV, COLS), F32),
        pltpu.SemaphoreType.DMA((10,)),
        pltpu.SemaphoreType.DMA((19,)),
        pltpu.SemaphoreType.DMA((19,)),
    ]
    to, mo, wr = pl.pallas_call(
        functools.partial(kernel, sizes),
        out_shape=(pltpu.VMEM(flat, F32), pltpu.VMEM(flat, F32), pltpu.VMEM((2 * LEV, 256), F32)),
        in_specs=[hbm] * 10,
        out_specs=(vmem, vmem, vmem),
        scratch_shapes=scratch,
        compiler_params=pltpu.CompilerParams(
            collective_id=0, has_side_effects=True, vmem_limit_bytes=67043328 - 640 * 1024
        ),
    )(cx, cy, k, d, sw, lw, t.reshape(flat), m.reshape(flat), flags.T, slots)
    to, mo, wr = pl.pallas_call(
        write_out,
        out_shape=tuple(jax.ShapeDtypeStruct(v.shape, F32) for v in (to, mo, wr)),
        in_specs=[vmem] * 3,
        out_specs=(hbm,) * 3,
        scratch_shapes=[pltpu.SemaphoreType.DMA((3,))],
        compiler_params=pltpu.CompilerParams(vmem_limit_bytes=1024 * 1024),
    )(to, mo, wr)
    return to.reshape(t.shape), mo.reshape(t.shape), wr.T


def solution(mesh):
    sizes = tuple(mesh.shape[a] for a in ("grp", "gx", "gy"))
    in_specs = (
        P("grp", "gx", "gy"), P("grp", "gx", "gy"),
        P(), P(), P(), P(), P(), P(),
        P(("grp", "gx", "gy"), None), P("gx", "gy"),
    )
    out_specs = (P("grp", "gx", "gy"), P("grp", "gx", "gy"), P(("grp", "gx", "gy"), None))
    return jax.shard_map(
        functools.partial(body, sizes), mesh=mesh, in_specs=in_specs, out_specs=out_specs, check_vma=False
    )
```

time: 69.2 us -> 42 us (0.61)
  the two profiles are of different devices: /device:TPU:1 before, /device:TPU:57 now
where the time goes in v1:
time: 42 us; the launch traced here: 41.9 us
  Pallas kernels  41.3 us (98%)
  between operations  0.64 us (2%)
    pallas_call x1, Pallas kernels, body(): pl.pallas_call(functools.partial(kernel, sizes), out_shape=(pltpu.VMEM(fl...  40.5 us

profile of v1, /device:TPU:57, one launch (start us, length us, event | category | flops | bytes accessed | tf_op | source)
XLA Modules:
  0.0 41.9 jit_solution(18266383068600983263)
XLA Ops:
  0.6 40.5 %shard_map.121 = (f32[512,128]{1,0:T(8,128)S(1)}, f32[512,128]{1,0:T(8,128)S(1)}, f32[64,256]{1,0:T(8,128)S(1)}) custom-call(f32[64]{0:T(128)} %cx_hbm.1, f32[64]{0:T(128)} %cy_hbm.1, f32[112]{0:T(128)} %k_hbm.1, f32[112]{0:T(128)} %d_hbm.1, f32[112]{0:T(128)} %sw_hbm.1, f32[112]{0:T(128)} %lw_hbm.1, f32[512,128]{1,0:T(8,128)} %bitcast.6, ...), custom_call_target="tpu_custom_call" | custom-call | tf_op jit(solution)/shard_map/pallas_call | solution.py:480
  41.1 0.8 %shard_map.122 = (f32[512,128]{1,0:T(8,128)}, f32[512,128]{1,0:T(8,128)}, f32[64,256]{1,0:T(8,128)}) custom-call(f32[512,128]{1,0:T(8,128)S(1)} %get-tuple-element.9.refs_0_, f32[512,128]{1,0:T(8,128)S(1)} %get-tuple-element.10.refs_1_, f32[64,256]{1,0:T(8,128)S(1)} %get-tuple-element.11.refs_2_), custom_call_target="tpu_custom_call" | custom-call | tf_op jit(solution)/shard_map/pallas_call | solution.py:490

commit v2 on v1

--- a/solution.py
+++ b/solution.py
@@ -48,7 +48,7 @@
     tin, min_, fin, sin,
     fs, es, coef, arad, crad, trad, acc, fsend, frecv, a0r, c0b,
     oh, fc, pws, wrecv, cus, ews, ewl, ewr,
-    eos, eol, eor, els, ell, elr, ehs, ehl, ehr, hst, hland,
+    eos, eol, eor, els, ell, elr, ehs, ehl, ehr, hst, hland, cst, cland, lland,
     load, send, recv,
 ):
     ng, nx, ny = sizes
@@ -97,17 +97,29 @@
     pl.semaphore_wait(barrier, len(peers))
 
     face = pl.ds(pl.multiple_of(DOWN - 8 - 24 * g, 8), H)
-    land = pl.ds(pl.multiple_of(8 + 40 * g, 8), H)
     first, last, mid = pl.ds(H, H), pl.ds(ROWS, H), pl.ds(H, ROWS)
     low, high = pl.ds(0, H), pl.ds(H + ROWS, H)
     levels_in = [
-        copy(4, fs.at[0, :, mid, face, :], fs.at[0, :, mid, land, :], (og, x, y)),
-        copy(5, fs.at[0, :, last, face, :], fs.at[0, :, low, land, :], (og, xn, y)),
-        copy(6, fs.at[0, :, first, face, :], fs.at[0, :, high, land, :], (og, xp, y)),
+        copy(4, fs.at[0, :, mid, face, :], lland, (og, x, y)),
+        copy(5, cst.at[0], cland.at[0], (og, xn, y)),
+        copy(6, cst.at[1], cland.at[1], (og, xp, y)),
     ]
     rows_low = copy(2, fs.at[0, :, last, own, :], fs.at[0, :, low, own, :], (g, xn, y))
     rows_high = copy(3, hst, hland, (g, xp, y))
-    for c in levels_in:
+    levels_in[0].start()
+
+    sub = subs((H, COLS))
+    for n in range(2):
+        for part in range(2):
+            def row(d, n=n, part=part):
+                return fs[0, part, 7 + d if n else 24 - d, face, :]
+
+            for d in range(1, 4):
+                first_group = jnp.where(sub >= d, row(d), roll(row(8 - d), d, 0))
+                second_group = jnp.where(sub < 8 - d, row(d), roll(row(8 - d), 8 - d, 0))
+                cst[n, 4 * part + d - 1] = jnp.where(g == 0, first_group, second_group)
+            cst[n, 4 * part + 3] = row(4)
+    for c in levels_in[1:]:
         c.start()
 
     for part in range(2):
@@ -177,14 +189,15 @@
             es[0, H + 4 * t + j, own, :] = roll(whole, -16 * j)
     rows_high.start()
 
-    dead = pl.ds(pl.multiple_of(8 + 40 * g, 8), H)
     zero8 = jnp.zeros((8, COLS), F32)
 
     def clear(r, _):
         for n in range(SWEEPS):
             for part in range(2):
-                fs[n, part, r, dead, :] = zero8
-            es[n, r, dead, :] = zero8
+                for side in (UP, DOWN):
+                    fs[n, part, r, side:side + H, :] = zero8
+            for side in (UP, DOWN):
+                es[n, r, side:side + H, :] = zero8
         return 0
 
     lax.fori_loop(0, XR, clear, 0)
@@ -193,6 +206,7 @@
         level = i + 24 * g
         hx, hy = 0.5 * cx_ref[level], 0.5 * cy_ref[level]
         for n, value in enumerate((NU_H - hx, NU_H + hx, NU_H - hy, NU_H + hy)):
+            value = value * (1.0 / NU_V)
             coef[n, pl.ds(OWN - 8 * g + i, 1), :] = jnp.full((1, COLS), value, F32)
         return 0
 
@@ -216,8 +230,8 @@
 
         def update(centre, nxt, prv, cols_n, cols_p, up_, down):
             return (
-                (1.0 - 4.0 * NU_H - 2.0 * NU_V) * centre + an * nxt + ap * prv
-                + bn * roll(cols_n, -1) + bp * roll(cols_p, 1) + NU_V * (up_ + down)
+                ((1.0 - 4.0 * NU_H - 2.0 * NU_V) / NU_V) * centre + an * nxt + ap * prv
+                + bn * roll(cols_n, -1) + bp * roll(cols_p, 1) + up_ + down
             )
 
         for j in range(count):
@@ -246,6 +260,43 @@
             return 0
 
         lax.fori_loop(0, count // each, block, 0)
+
+    lo = pl.multiple_of(OWN - 8 * g, 8)
+
+    def inner_rows(at, n):
+        for sweep in range(1, SWEEPS):
+            count = ROWS - 2 * sweep
+            blocks(sweep, at, n, H + sweep, count, {14: 7, 12: 6, 10: 5, 8: 4, 6: 6, 4: 4, 2: 2}[count])
+
+    inner_rows(OWN, LEV)
+
+    for c in levels_in:
+        c.wait_recv()
+    arrived = pl.ds(pl.multiple_of(DOWN - 40 * g, 8), H)
+
+    for part in range(2):
+        for r in range(ROWS):
+            fs[0, part, H + r, arrived, :] = lland[part, r]
+    for n in range(2):
+        for part in range(2):
+            def put(d, value, n=n, part=part):
+                fs[0, part, 23 + d if n else 8 - d, arrived, :] = value
+
+            for d in range(1, 4):
+                both = cland[n, 4 * part + d - 1]
+                put(d, both)
+                put(8 - d, jnp.where(g == 1, roll(both, 8 - d, 0), roll(both, d, 0)))
+            for d in (4, 8):
+                put(d, cland[n, 4 * part + 3])
+
+    def pack_levels(t, _):
+        els[t] = pack(4 * t, arrived, H)
+        return 0
+
+    lax.fori_loop(0, XR // 4, pack_levels, 0)
+    edges_lev = [copy(1, els, ell, (g, x, yn)), copy(11, els, elr, (g, x, yp))]
+    for c in edges_lev:
+        c.start()
 
     clouds.wait_recv()
     fc[0:LEV, pl.ds(mine, 256)] = fin[pl.ds(pl.multiple_of(LEV * g, 8), LEV), :].astype(F32)
@@ -330,19 +381,6 @@
     back.start()
     wr_ref[pl.ds(pl.multiple_of(LEV * g, 8), LEV), :] = pws[:, pl.ds(mine, 256)]
 
-    for c in levels_in:
-        c.wait_recv()
-    arrived = pl.ds(pl.multiple_of(DOWN - 40 * g, 8), H)
-
-    def pack_levels(t, _):
-        els[t] = pack(4 * t, arrived, H)
-        return 0
-
-    lax.fori_loop(0, XR // 4, pack_levels, 0)
-    edges_lev = [copy(1, els, ell, (g, x, yn)), copy(11, els, elr, (g, x, yp))]
-    for c in edges_lev:
-        c.start()
-
     edge_rows = []
 
     def offer():
@@ -389,11 +427,9 @@
         return 0
 
     lax.fori_loop(0, XR // 4, settle, 0)
-    lo = pl.multiple_of(OWN - 8 * g, 8)
-
-    for sweep in range(1, SWEEPS):
-        count = ROWS - 2 * sweep
-        blocks(sweep, lo, LEV + H, H + sweep, count, {14: 7, 12: 6, 10: 5, 8: 4, 6: 6, 4: 4, 2: 2}[count])
+
+    reach = pl.multiple_of(DOWN - 8 - 32 * g, 8)
+    inner_rows(reach, 2 * H)
     take()
     sweep_side(0)
     rows_high.wait_recv()
@@ -413,8 +449,8 @@
         for half in range(2):
             r = 2 * i + half
             heat = 0.75 * cus[1 + i] + 0.25 * cus[i + 2 * half]
-            to_ref[pl.ds(r, LEV, stride=ROWS), :] = fs[SWEEPS, 0, H + r, own, :] + HEATING_INTERVAL * heat
-            mo_ref[pl.ds(r, LEV, stride=ROWS), :] = roll(fs[SWEEPS, 1, H + r, own, :], 64)
+            to_ref[pl.ds(r, LEV, stride=ROWS), :] = NU_V ** SWEEPS * fs[SWEEPS, 0, H + r, own, :] + HEATING_INTERVAL * heat
+            mo_ref[pl.ds(r, LEV, stride=ROWS), :] = roll(NU_V ** SWEEPS * fs[SWEEPS, 1, H + r, own, :], 64)
         return 0
 
     lax.fori_loop(0, ROWS // 2, finish, 0)
@@ -473,6 +509,9 @@
         pltpu.VMEM((2, LEV, COLS), F32),
         pltpu.VMEM((2 * H + 2, LEV, COLS), F32),
         pltpu.VMEM((2 * H + 2, LEV, COLS), F32),
+        pltpu.VMEM((2, 8, H, COLS), F32),
+        pltpu.VMEM((2, 8, H, COLS), F32),
+        pltpu.VMEM((2, ROWS, H, COLS), F32),
         pltpu.SemaphoreType.DMA((10,)),
         pltpu.SemaphoreType.DMA((19,)),
         pltpu.SemaphoreType.DMA((19,)),

time: 42 us -> 39.3 us (0.936)
  the two profiles are of different devices: /device:TPU:57 before, /device:TPU:1 now
where the time goes in v2:
time: 39.3 us; the launch traced here: 39.2 us
  Pallas kernels  38.5 us (98%)
  between operations  0.64 us (2%)
    pallas_call x1, Pallas kernels, body(): pl.pallas_call(functools.partial(kernel, sizes), out_shape=(pltpu.VMEM(fl...  37.7 us
    pallas_call x1, Pallas kernels, body(): pl.pallas_call(write_out, out_shape=tuple((jax.ShapeDtypeStruct(v.shape,...  0.83 us

profile of v2, /device:TPU:1, one launch (start us, length us, event | category | flops | bytes accessed | tf_op | source)
XLA Modules:
  0.0 39.2 jit_solution(11807799415836101443)
XLA Ops:
  0.6 37.7 %shard_map.121 = (f32[512,128]{1,0:T(8,128)S(1)}, f32[512,128]{1,0:T(8,128)S(1)}, f32[64,256]{1,0:T(8,128)S(1)}) custom-call(f32[64]{0:T(128)} %cx_hbm.1, f32[64]{0:T(128)} %cy_hbm.1, f32[112]{0:T(128)} %k_hbm.1, f32[112]{0:T(128)} %d_hbm.1, f32[112]{0:T(128)} %sw_hbm.1, f32[112]{0:T(128)} %lw_hbm.1, f32[512,128]{1,0:T(8,128)} %bitcast.6, ...), custom_call_target="tpu_custom_call" | custom-call | tf_op jit(solution)/shard_map/pallas_call | solution.py:519
  38.3 0.8 %shard_map.122 = (f32[512,128]{1,0:T(8,128)}, f32[512,128]{1,0:T(8,128)}, f32[64,256]{1,0:T(8,128)}) custom-call(f32[512,128]{1,0:T(8,128)S(1)} %get-tuple-element.9.refs_0_, f32[512,128]{1,0:T(8,128)S(1)} %get-tuple-element.10.refs_1_, f32[64,256]{1,0:T(8,128)S(1)} %get-tuple-element.11.refs_2_), custom_call_target="tpu_custom_call" | custom-call | tf_op jit(solution)/shard_map/pallas_call | solution.py:529

commit v3 on v2

--- a/solution.py
+++ b/solution.py
@@ -48,7 +48,7 @@
     tin, min_, fin, sin,
     fs, es, coef, arad, crad, trad, acc, fsend, frecv, a0r, c0b,
     oh, fc, pws, wrecv, cus, ews, ewl, ewr,
-    eos, eol, eor, els, ell, elr, ehs, ehl, ehr, hst, hland, cst, cland, lland,
+    eos, eol, eor, els, ell, elr, hst, hland, cst, cland, lland,
     load, send, recv,
 ):
     ng, nx, ny = sizes
@@ -97,16 +97,14 @@
     pl.semaphore_wait(barrier, len(peers))
 
     face = pl.ds(pl.multiple_of(DOWN - 8 - 24 * g, 8), H)
-    first, last, mid = pl.ds(H, H), pl.ds(ROWS, H), pl.ds(H, ROWS)
-    low, high = pl.ds(0, H), pl.ds(H + ROWS, H)
+    mid = pl.ds(H, ROWS)
     levels_in = [
         copy(4, fs.at[0, :, mid, face, :], lland, (og, x, y)),
         copy(5, cst.at[0], cland.at[0], (og, xn, y)),
         copy(6, cst.at[1], cland.at[1], (og, xp, y)),
     ]
-    rows_low = copy(2, fs.at[0, :, last, own, :], fs.at[0, :, low, own, :], (g, xn, y))
-    rows_high = copy(3, hst, hland, (g, xp, y))
-    levels_in[0].start()
+    rows_low = copy(2, hst.at[0], hland.at[0], (g, xn, y))
+    rows_high = copy(3, hst.at[1], hland.at[1], (g, xp, y))
 
     sub = subs((H, COLS))
     for n in range(2):
@@ -124,7 +122,8 @@
 
     for part in range(2):
         for r in range(H):
-            hst[H * part + r] = fs[0, part, H + r, own, :]
+            hst[0, H * part + r] = fs[0, part, ROWS + r, own, :]
+            hst[1, H * part + r] = fs[0, part, H + r, own, :]
 
     lane = lanes((LEV, COLS))
     outer = (lane < 8) | (lane >= COLS - 8)
@@ -176,18 +175,18 @@
     fsend[LEV:LEV + 1, COLS:2 * COLS] = below[:, 0:COLS]
     fsend[LEV + 1:LEV + 2, COLS:2 * COLS] = below[:, COLS:256]
     clouds = copy(0, fsend, frecv, (og, x, y))
-    for c in [clouds, rows_low]:
+    for c in [clouds, levels_in[0]]:
         c.start()
 
     for c in edges_own:
         c.wait_recv()
     for t in range(4):
         whole = jnp.where(from_left, eol[t], eor[t])
-        if t < 2:
-            hst[2 * H + t] = whole
+        hst[1 - t // 2, 2 * H + t % 2] = whole
         for j in range(4):
             es[0, H + 4 * t + j, own, :] = roll(whole, -16 * j)
-    rows_high.start()
+    for c in (rows_low, rows_high):
+        c.start()
 
     zero8 = jnp.zeros((8, COLS), F32)
 
@@ -269,34 +268,6 @@
             blocks(sweep, at, n, H + sweep, count, {14: 7, 12: 6, 10: 5, 8: 4, 6: 6, 4: 4, 2: 2}[count])
 
     inner_rows(OWN, LEV)
-
-    for c in levels_in:
-        c.wait_recv()
-    arrived = pl.ds(pl.multiple_of(DOWN - 40 * g, 8), H)
-
-    for part in range(2):
-        for r in range(ROWS):
-            fs[0, part, H + r, arrived, :] = lland[part, r]
-    for n in range(2):
-        for part in range(2):
-            def put(d, value, n=n, part=part):
-                fs[0, part, 23 + d if n else 8 - d, arrived, :] = value
-
-            for d in range(1, 4):
-                both = cland[n, 4 * part + d - 1]
-                put(d, both)
-                put(8 - d, jnp.where(g == 1, roll(both, 8 - d, 0), roll(both, d, 0)))
-            for d in (4, 8):
-                put(d, cland[n, 4 * part + 3])
-
-    def pack_levels(t, _):
-        els[t] = pack(4 * t, arrived, H)
-        return 0
-
-    lax.fori_loop(0, XR // 4, pack_levels, 0)
-    edges_lev = [copy(1, els, ell, (g, x, yn)), copy(11, els, elr, (g, x, yp))]
-    for c in edges_lev:
-        c.start()
 
     clouds.wait_recv()
     fc[0:LEV, pl.ds(mine, 256)] = fin[pl.ds(pl.multiple_of(LEV * g, 8), LEV), :].astype(F32)
@@ -378,32 +349,49 @@
         total = part if total is None else total + part
     pws[...] = total
     back = copy(14, pws.at[:, pl.ds(theirs, 256)], wrecv, (og, x, y))
-    back.start()
     wr_ref[pl.ds(pl.multiple_of(LEV * g, 8), LEV), :] = pws[:, pl.ds(mine, 256)]
 
-    edge_rows = []
-
-    def offer():
+    for c in levels_in:
+        c.wait_recv()
+    arrived = pl.ds(pl.multiple_of(DOWN - 40 * g, 8), H)
+
+    for part in range(2):
+        for r in range(ROWS):
+            fs[0, part, H + r, arrived, :] = lland[part, r]
+    for n in range(2):
+        for part in range(2):
+            def put(d, value, n=n, part=part):
+                fs[0, part, 23 + d if n else 8 - d, arrived, :] = value
+
+            for d in range(1, 4):
+                both = cland[n, 4 * part + d - 1]
+                put(d, both)
+                put(8 - d, jnp.where(g == 1, roll(both, 8 - d, 0), roll(both, d, 0)))
+            for d in (4, 8):
+                put(d, cland[n, 4 * part + 3])
+
+    def pack_levels(t, _):
+        els[t] = pack(4 * t, arrived, H)
+        return 0
+
+    lax.fori_loop(0, XR // 4, pack_levels, 0)
+    edges_lev = [copy(1, els, ell, (g, x, yn)), copy(11, els, elr, (g, x, yp))]
+    for c in edges_lev:
+        c.start()
+
+    def take(n):
+        for r in range(H):
+            for part in range(2):
+                fs[0, part, n * (H + ROWS) + r, own, :] = hland[n, H * part + r]
         for t in range(2):
-            ehs[t] = pack(4 * t)
-        for i, dst, peer in ((9, ehl, (g, x, yn)), (10, ehr, (g, x, yp))):
-            edge_rows.append(copy(i, ehs, dst, peer))
-            edge_rows[-1].start()
-
-    def take():
-        for c in edge_rows:
-            c.wait_recv()
-        for t in range(2):
-            whole = jnp.where(from_left, ehl[t], ehr[t])
+            whole = hland[n, 2 * H + t]
             for j in range(4):
-                es[0, 4 * t + j, own, :] = roll(whole, -16 * j)
+                es[0, n * (H + ROWS) + 4 * t + j, own, :] = roll(whole, -16 * j)
 
     def sweep_side(n):
         for sweep in range(1, SWEEPS + 1):
             advance(sweep, lo, LEV + H, XR - sweep - H if n else sweep, H)
 
-    rows_low.wait_recv()
-    offer()
 
     for c in ends:
         c.wait_recv()
@@ -414,7 +402,7 @@
         line = line + jnp.where(lane == COLS - 1, roll(right, COLS - 1 - 2 * i), 0.0)
         cus[1 + i] = line
     lines = [copy(15, cus.at[8], cus.at[0], (g, xn, y)), copy(16, cus.at[1], cus.at[9], (g, xp, y))]
-    for c in lines:
+    for c in [*lines, back]:
         c.start()
 
     for c in edges_lev:
@@ -430,16 +418,11 @@
 
     reach = pl.multiple_of(DOWN - 8 - 32 * g, 8)
     inner_rows(reach, 2 * H)
-    take()
+    rows_low.wait_recv()
+    take(0)
     sweep_side(0)
     rows_high.wait_recv()
-    for r in range(H):
-        for part in range(2):
-            fs[0, part, H + ROWS + r, own, :] = hland[H * part + r]
-    for t in range(2):
-        whole = hland[2 * H + t]
-        for j in range(4):
-            es[0, H + ROWS + 4 * t + j, own, :] = roll(whole, -16 * j)
+    take(1)
     sweep_side(1)
 
     for c in lines:
@@ -457,7 +440,7 @@
 
     back.wait_recv()
     wr_ref[pl.ds(pl.multiple_of(LEV * og, 8), LEV), :] = wrecv[...]
-    for c in [clouds, rows_low, rows_high, *levels_in, *edges_own, *edge_rows, *edges_lev, *ends, back, *lines]:
+    for c in [clouds, rows_low, rows_high, *levels_in, *edges_own, *edges_lev, *ends, back, *lines]:
         c.wait_send()
 
 
@@ -504,11 +487,8 @@
         pltpu.VMEM((8, H, COLS), F32),
         pltpu.VMEM((8, H, COLS), F32),
         pltpu.VMEM((8, H, COLS), F32),
-        pltpu.VMEM((2, LEV, COLS), F32),
-        pltpu.VMEM((2, LEV, COLS), F32),
-        pltpu.VMEM((2, LEV, COLS), F32),
-        pltpu.VMEM((2 * H + 2, LEV, COLS), F32),
-        pltpu.VMEM((2 * H + 2, LEV, COLS), F32),
+        pltpu.VMEM((2, 2 * H + 2, LEV, COLS), F32),
+        pltpu.VMEM((2, 2 * H + 2, LEV, COLS), F32),
         pltpu.VMEM((2, 8, H, COLS), F32),
         pltpu.VMEM((2, 8, H, COLS), F32),
         pltpu.VMEM((2, ROWS, H, COLS), F32),

time: 39.3 us -> 38.6 us (0.982)
  Pallas kernels: 38.5 us -> 37.9 us
    pallas_call x1, Pallas kernels: 37.7 us -> 37 us  [body(): pl.pallas_call(functools.partial(kernel, sizes), out_shape=(pltpu.VMEM(fl...]
where the time goes in v3:
time: 38.6 us; the launch traced here: 38.5 us
  Pallas kernels  37.9 us (98%)
  between operations  0.64 us (2%)
    pallas_call x1, Pallas kernels, body(): pl.pallas_call(functools.partial(kernel, sizes), out_shape=(pltpu.VMEM(fl...  37 us
    pallas_call x1, Pallas kernels, body(): pl.pallas_call(write_out, out_shape=tuple((jax.ShapeDtypeStruct(v.shape,...  0.83 us

profile of v3, /device:TPU:1, one launch (start us, length us, event | category | flops | bytes accessed | tf_op | source)
XLA Modules:
  0.0 38.5 jit_solution(13348090305380573904)
XLA Ops:
  0.6 37.0 %shard_map.121 = (f32[512,128]{1,0:T(8,128)S(1)}, f32[512,128]{1,0:T(8,128)S(1)}, f32[64,256]{1,0:T(8,128)S(1)}) custom-call(f32[64]{0:T(128)} %cx_hbm.1, f32[64]{0:T(128)} %cy_hbm.1, f32[112]{0:T(128)} %k_hbm.1, f32[112]{0:T(128)} %d_hbm.1, f32[112]{0:T(128)} %sw_hbm.1, f32[112]{0:T(128)} %lw_hbm.1, f32[512,128]{1,0:T(8,128)} %bitcast.6, ...), custom_call_target="tpu_custom_call" | custom-call | tf_op jit(solution)/shard_map/pallas_call | solution.py:499
  37.7 0.8 %shard_map.122 = (f32[512,128]{1,0:T(8,128)}, f32[512,128]{1,0:T(8,128)}, f32[64,256]{1,0:T(8,128)}) custom-call(f32[512,128]{1,0:T(8,128)S(1)} %get-tuple-element.9.refs_0_, f32[512,128]{1,0:T(8,128)S(1)} %get-tuple-element.10.refs_1_, f32[64,256]{1,0:T(8,128)S(1)} %get-tuple-element.11.refs_2_), custom_call_target="tpu_custom_call" | custom-call | tf_op jit(solution)/shard_map/pallas_call | solution.py:509

commit v4 on v3

--- a/solution.py
+++ b/solution.py
@@ -351,48 +351,6 @@
     back = copy(14, pws.at[:, pl.ds(theirs, 256)], wrecv, (og, x, y))
     wr_ref[pl.ds(pl.multiple_of(LEV * g, 8), LEV), :] = pws[:, pl.ds(mine, 256)]
 
-    for c in levels_in:
-        c.wait_recv()
-    arrived = pl.ds(pl.multiple_of(DOWN - 40 * g, 8), H)
-
-    for part in range(2):
-        for r in range(ROWS):
-            fs[0, part, H + r, arrived, :] = lland[part, r]
-    for n in range(2):
-        for part in range(2):
-            def put(d, value, n=n, part=part):
-                fs[0, part, 23 + d if n else 8 - d, arrived, :] = value
-
-            for d in range(1, 4):
-                both = cland[n, 4 * part + d - 1]
-                put(d, both)
-                put(8 - d, jnp.where(g == 1, roll(both, 8 - d, 0), roll(both, d, 0)))
-            for d in (4, 8):
-                put(d, cland[n, 4 * part + 3])
-
-    def pack_levels(t, _):
-        els[t] = pack(4 * t, arrived, H)
-        return 0
-
-    lax.fori_loop(0, XR // 4, pack_levels, 0)
-    edges_lev = [copy(1, els, ell, (g, x, yn)), copy(11, els, elr, (g, x, yp))]
-    for c in edges_lev:
-        c.start()
-
-    def take(n):
-        for r in range(H):
-            for part in range(2):
-                fs[0, part, n * (H + ROWS) + r, own, :] = hland[n, H * part + r]
-        for t in range(2):
-            whole = hland[n, 2 * H + t]
-            for j in range(4):
-                es[0, n * (H + ROWS) + 4 * t + j, own, :] = roll(whole, -16 * j)
-
-    def sweep_side(n):
-        for sweep in range(1, SWEEPS + 1):
-            advance(sweep, lo, LEV + H, XR - sweep - H if n else sweep, H)
-
-
     for c in ends:
         c.wait_recv()
     left, right = ewl[...] * (1.0 / 3.0), ewr[...] * (1.0 / 3.0)
@@ -402,8 +360,50 @@
         line = line + jnp.where(lane == COLS - 1, roll(right, COLS - 1 - 2 * i), 0.0)
         cus[1 + i] = line
     lines = [copy(15, cus.at[8], cus.at[0], (g, xn, y)), copy(16, cus.at[1], cus.at[9], (g, xp, y))]
-    for c in [*lines, back]:
-        c.start()
+    for c in lines:
+        c.start()
+
+    for c in levels_in:
+        c.wait_recv()
+    arrived = pl.ds(pl.multiple_of(DOWN - 40 * g, 8), H)
+
+    for part in range(2):
+        for r in range(ROWS):
+            fs[0, part, H + r, arrived, :] = lland[part, r]
+    for n in range(2):
+        for part in range(2):
+            def put(d, value, n=n, part=part):
+                fs[0, part, 23 + d if n else 8 - d, arrived, :] = value
+
+            for d in range(1, 4):
+                both = cland[n, 4 * part + d - 1]
+                put(d, both)
+                put(8 - d, jnp.where(g == 1, roll(both, 8 - d, 0), roll(both, d, 0)))
+            for d in (4, 8):
+                put(d, cland[n, 4 * part + 3])
+
+    def pack_levels(t, _):
+        els[t] = pack(4 * t, arrived, H)
+        return 0
+
+    lax.fori_loop(0, XR // 4, pack_levels, 0)
+    edges_lev = [copy(1, els, ell, (g, x, yn)), copy(11, els, elr, (g, x, yp))]
+    for c in edges_lev:
+        c.start()
+
+    def take(n):
+        for r in range(H):
+            for part in range(2):
+                fs[0, part, n * (H + ROWS) + r, own, :] = hland[n, H * part + r]
+        for t in range(2):
+            whole = hland[n, 2 * H + t]
+            for j in range(4):
+                es[0, n * (H + ROWS) + 4 * t + j, own, :] = roll(whole, -16 * j)
+
+    def sweep_side(n):
+        for sweep in range(1, SWEEPS + 1):
+            advance(sweep, lo, LEV + H, XR - sweep - H if n else sweep, H)
+
 
     for c in edges_lev:
         c.wait_recv()
@@ -419,24 +419,32 @@
     reach = pl.multiple_of(DOWN - 8 - 32 * g, 8)
     inner_rows(reach, 2 * H)
     rows_low.wait_recv()
+    back.start()
     take(0)
     sweep_side(0)
     rows_high.wait_recv()
     take(1)
     sweep_side(1)
 
+    def finish_moisture(i, _):
+        for half in range(8):
+            r = 8 * i + half
+            mo_ref[pl.ds(r, LEV, stride=ROWS), :] = roll(NU_V ** SWEEPS * fs[SWEEPS, 1, H + r, own, :], 64)
+        return 0
+
+    lax.fori_loop(0, ROWS // 8, finish_moisture, 0)
     for c in lines:
         c.wait_recv()
 
-    def finish(i, _):
-        for half in range(2):
+    def finish(b, _):
+        for n in range(8):
+            i, half = 4 * b + n // 2, n % 2
             r = 2 * i + half
             heat = 0.75 * cus[1 + i] + 0.25 * cus[i + 2 * half]
             to_ref[pl.ds(r, LEV, stride=ROWS), :] = NU_V ** SWEEPS * fs[SWEEPS, 0, H + r, own, :] + HEATING_INTERVAL * heat
-            mo_ref[pl.ds(r, LEV, stride=ROWS), :] = roll(NU_V ** SWEEPS * fs[SWEEPS, 1, H + r, own, :], 64)
-        return 0
-
-    lax.fori_loop(0, ROWS // 2, finish, 0)
+        return 0
+
+    lax.fori_loop(0, ROWS // 8, finish, 0)
 
     back.wait_recv()
     wr_ref[pl.ds(pl.multiple_of(LEV * og, 8), LEV), :] = wrecv[...]

time: 38.6 us -> 38 us (0.984)
  Pallas kernels: 37.9 us -> 37.3 us
    pallas_call x1, Pallas kernels: 37 us -> 36.4 us  [body(): pl.pallas_call(functools.partial(kernel, sizes), out_shape=(pltpu.VMEM(fl...]
where the time goes in v4:
time: 38 us; the launch traced here: 37.9 us
  Pallas kernels  37.3 us (98%)
  between operations  0.64 us (2%)
    pallas_call x1, Pallas kernels, body(): pl.pallas_call(functools.partial(kernel, sizes), out_shape=(pltpu.VMEM(fl...  36.4 us
    pallas_call x1, Pallas kernels, body(): pl.pallas_call(write_out, out_shape=tuple((jax.ShapeDtypeStruct(v.shape,...  0.83 us

profile of v4, /device:TPU:1, one launch (start us, length us, event | category | flops | bytes accessed | tf_op | source)
XLA Modules:
  0.0 37.9 jit_solution(8732569768705158280)
XLA Ops:
  0.6 36.4 %shard_map.121 = (f32[512,128]{1,0:T(8,128)S(1)}, f32[512,128]{1,0:T(8,128)S(1)}, f32[64,256]{1,0:T(8,128)S(1)}) custom-call(f32[64]{0:T(128)} %cx_hbm.1, f32[64]{0:T(128)} %cy_hbm.1, f32[112]{0:T(128)} %k_hbm.1, f32[112]{0:T(128)} %d_hbm.1, f32[112]{0:T(128)} %sw_hbm.1, f32[112]{0:T(128)} %lw_hbm.1, f32[512,128]{1,0:T(8,128)} %bitcast.6, ...), custom_call_target="tpu_custom_call" | custom-call | tf_op jit(solution)/shard_map/pallas_call | solution.py:507
  37.1 0.8 %shard_map.122 = (f32[512,128]{1,0:T(8,128)}, f32[512,128]{1,0:T(8,128)}, f32[64,256]{1,0:T(8,128)}) custom-call(f32[512,128]{1,0:T(8,128)S(1)} %get-tuple-element.9.refs_0_, f32[512,128]{1,0:T(8,128)S(1)} %get-tuple-element.10.refs_1_, f32[64,256]{1,0:T(8,128)S(1)} %get-tuple-element.11.refs_2_), custom_call_target="tpu_custom_call" | custom-call | tf_op jit(solution)/shard_map/pallas_call | solution.py:517
